TPU v7x, 256 devices: a whole 4x4x8 slice. The times are simulated.
256 devices in a mesh: rows: 32 (over z, y_lo, core), cols: 8 (over x, y_hi).
Axes of the slice: x: 4, y: 4 (y_hi: 2, y_lo: 2; y = y_hi * 2 + y_lo), z: 8, core: 2. Of those that a mesh axis runs over, the one named last changes fastest.
Arguments:
- matrix: float32 [8192, 8192], P('rows', 'cols'), may hold values from -6 to 6
- starts: int32 [4, 4], replicated, may hold values from 0 to 7936, as said below
- factors: float32 [4, 4, 256, 256], P(None, None, 'rows', 'cols'), as said below
Outputs:
- updated: float32 [8192, 8192], P('rows', 'cols')
Inputs may be any that keep to these rules, and one draw needn't show every extreme that they name: `starts`: every start is a multiple of 128; chain c's start lies in the c-th of 4 equal ranges of blocks and never decreases from advance to advance; a window may end on the first block of the next range; the windows of one advance are disjoint. `factors`: every factor is orthogonal.
All inputs are finite; a program needn't handle non-finite values.
Results may differ from a plain program's by a relative error of at most 0.0001.
Values sent between devices are 32-bit elements; how exact they have to be, the bound alone decides.
No kernel may reach another device: no remote copies, remote signals or barrier semaphores. Data moves between devices by JAX's collectives and lax.ppermute only.
A program may use at most 64 MiB of HBM per device.

v0:
```python
import jax
import jax.numpy as jnp
from jax import lax
from jax.experimental import pallas as pl
from jax.experimental.pallas import tpu as pltpu
from jax.sharding import Mesh
from jax.sharding import PartitionSpec as P


NB = 128
CHAINS = 4
ADV = 4
PLANES = 8
QUADS = 4
COLS = 8
EACH = 32
WIDE = 256


def pieces_kernel(factors, out):
    for half in range(2):
        pieces = [factors[2 * half + a, c] for a in range(2) for c in range(CHAINS)]
        piece = jnp.concatenate(pieces, axis=1)
        for d in range(half, PLANES * QUADS, 2):
            out[d] = piece


def gather_kernel(place, b0, b1, b2, b3, out, low):
    for m, block in enumerate((b0, b1, b2, b3)):
        out[place[1] ^ m] = block[...]
    low[...] = out[:2]


def spread_kernel(pieces, out):
    turned = pieces[...].reshape(WIDE, WIDE).T
    for e in range(COLS):
        out[e] = turned


def split(x):
    high = x.astype(jnp.bfloat16)
    return high, (x - high.astype(jnp.float32)).astype(jnp.bfloat16)


def turned_factor(k, c, core, own, other):
    at = ((k % 2) * CHAINS + c) * 32
    picked = jnp.where(core == k // 2, own[:, at : at + 32, :], other[:, at : at + 32, :])
    return split(picked.reshape(WIDE, WIDE))


def dot(a, b, b_dim):
    return lax.dot_general(a, b, (((1,), (b_dim,)), ((), ())), preferred_element_type=jnp.float32)


def row_pass(panel, plane, first, last, starts, core, own, other):
    for k in range(ADV):
        for c in range(CHAINS):
            offset = lax.div(starts[k, c], NB) + 1 - QUADS * plane
            slot = (offset >= PLANES * QUADS).astype(jnp.int32)
            head = offset - PLANES * QUADS * slot

            @pl.when((head >= first) & (head <= last))
            def _():
                f_high, f_low = turned_factor(k, c, core, own, other)
                window = jnp.concatenate([panel[head, slot], panel[head + 1, slot]], axis=0)
                w_high, w_low = split(window)
                new = dot(f_high, w_high, 0) + (dot(f_low, w_high, 0) + dot(f_high, w_low, 0))
                panel[head, slot] = new[:NB]
                panel[head + 1, slot] = new[NB:]


def crossing(starts, first_block):
    found = jnp.int32(0)
    for k in range(ADV):
        for c in range(CHAINS):
            head = lax.div(starts[k, c], NB) + 1
            near = (head == first_block) | (head == first_block + PLANES * QUADS)
            found = found | near.astype(jnp.int32)
    return found == 1


def row_kernel(starts, place, lower, middle, upper, own, other, out, panel, side):
    core, plane = place[0], place[2]
    below = lax.rem(plane + PLANES - 1, PLANES)
    above = lax.rem(plane + 1, PLANES)
    into = crossing(starts, QUADS * plane)
    out_of = crossing(starts, QUADS * plane + QUADS)
    shift_low = (plane == 0).astype(jnp.int32)
    shift_high = (plane == PLANES - 1).astype(jnp.int32)

    @pl.when(into | (plane == 0))
    def _():
        side[1:5] = lower[...]
        row_pass(side, below, 1, 3, starts, core, own, other)
        panel[0, 0] = side[4, 0]
        panel[0, 1] = side[4, 1 - shift_low]

    @pl.when(out_of | (plane == PLANES - 1))
    def _():
        side[1:3] = upper[...]

        @pl.when(lax.rem(above, PLANES // 2) == 0)
        def _():
            row_pass(side, above, 1, 1, starts, core, own, other)

        panel[5, 0] = side[1, shift_high]
        panel[5, 1] = side[1, 1]

    panel[1:5] = middle[...]
    row_pass(panel, plane, 0, 4, starts, core, own, other)
    out[...] = panel[1:5]


def col_kernel(starts, place, data, own, other, out):
    for q in range(QUADS):
        out[:, :, q * WIDE : (q + 1) * WIDE] = data[q]

    def spot(block):
        return lax.rem(block, COLS), pl.multiple_of(lax.div(block, COLS) * NB, NB)

    for k in range(ADV):
        results = []
        for c in range(CHAINS):
            head = lax.div(starts[k, c], NB)
            e0, o0 = spot(head)
            e1, o1 = spot(head + 1)
            window = jnp.concatenate([out[e0, :, pl.ds(o0, NB)], out[e1, :, pl.ds(o1, NB)]], axis=1)
            w_high, w_low = split(window)
            f_high, f_low = turned_factor(k, c, place[0], own, other)
            both = dot(jnp.concatenate([w_high, w_low], axis=0), f_high, 1)
            new = both[:EACH] + (both[EACH:] + dot(w_high, f_low, 1))
            results.append((e0, o0, e1, o1, new))
        for e0, o0, e1, o1, new in results:
            out[e0, :, pl.ds(o0, NB)] = new[:, :NB]
            out[e1, :, pl.ds(o1, NB)] = new[:, NB:]


SCALARS = pl.BlockSpec(memory_space=pltpu.SMEM)
VALUES = pl.BlockSpec(memory_space=pltpu.VMEM)


def kernel(body, scalars, inputs, out_shapes, scratch=()):
    outs = [jax.ShapeDtypeStruct(shape, jnp.float32) for shape in out_shapes]
    return pl.pallas_call(
        body,
        in_specs=[SCALARS] * scalars + [VALUES] * inputs,
        out_specs=[VALUES] * len(outs),
        out_shape=outs,
        scratch_shapes=[pltpu.VMEM(shape, jnp.float32) for shape in scratch],
        compiler_params=pltpu.CompilerParams(vmem_limit_bytes=24 << 20),
    )


def local(matrix, starts, factors):
    z = lax.axis_index("planes")
    q = lax.axis_index("quads")
    place = jnp.stack([lax.rem(q, 2), q, z])
    (sent,) = kernel(pieces_kernel, 0, 1, [(PLANES * QUADS, 8, WIDE)])(factors)
    got = lax.all_to_all(sent, ("planes", "quads"), 0, 0, tiled=True)
    tile = matrix.reshape(2, NB, QUADS * WIDE)
    quarters = [lax.dynamic_slice_in_dim(tile, (q ^ m) * WIDE, WIDE, 2) for m in range(QUADS)]
    blocks = [quarters[0]]
    for m in range(1, QUADS):
        blocks.append(lax.ppermute(quarters[m], "quads", [(i, i ^ m) for i in range(QUADS)]))
    (sent,) = kernel(spread_kernel, 0, 1, [(COLS, WIDE, WIDE)])(got)
    own = lax.all_to_all(sent, "cols", 0, 0, tiled=True)
    panel = (QUADS, 2, NB, WIDE)
    middle, low = kernel(gather_kernel, 1, 4, [panel, (2, 2, NB, WIDE)])(place, *blocks)
    lower = lax.ppermute(middle, "planes", [(i, (i + 1) % PLANES) for i in range(PLANES)])
    upper = lax.ppermute(low, "planes", [(i, (i - 1) % PLANES) for i in range(PLANES)])
    other = lax.ppermute(own, "quads", [(i, i ^ 1) for i in range(QUADS)])
    wide = [(QUADS + 2, 2, NB, WIDE), (QUADS + 1, 2, NB, WIDE)]
    (rows,) = kernel(row_kernel, 2, 5, [panel], wide)(
        starts, place, lower, middle, upper, own, other
    )
    rows = rows.reshape(QUADS * COLS, EACH, WIDE)
    came = lax.all_to_all(rows, ("quads", "cols"), 0, 0, tiled=True)
    came = came.reshape(QUADS, COLS, EACH, WIDE)
    (done,) = kernel(col_kernel, 2, 3, [(COLS, EACH, QUADS * WIDE)])(
        starts, place, came, own, other
    )
    home = lax.all_to_all(done, "cols", 0, 0, tiled=True)
    return home.reshape(2 * NB, QUADS * WIDE)


def solution(mesh):
    finer = Mesh(mesh.devices.reshape(PLANES, QUADS, COLS), ("planes", "quads", "cols"))
    rows = ("planes", "quads")
    in_specs = (P(rows, "cols"), P(), P(None, None, rows, "cols"))
    return jax.shard_map(
        local, mesh=finer, in_specs=in_specs, out_specs=P(rows, "cols"), check_vma=False
    )
```

profile of v0, /device:TPU:8, one launch (start us, length us, event | category | flops | bytes accessed | tf_op | source)
XLA Modules:
  0.0 147.8 jit_solution(15788148556112076771)
XLA Ops:
  0.0 0.0 copy-start
  0.0 0.8 copy-done
  0.8 0.1 shard_map.38
  0.9 21.9 %all_to_all.20.pieces = f32[32,8,256]{2,1,0:T(8,128)S(1)} all-to-all(f32[32,8,256]{2,1,0:T(8,128)S(1)} %shard_map.38), channel_id=1, replica_groups=mesh['planes'=8,'quads'=4,'cols'=8] {'planes','quads'}, dimensions={0} | all-to-all | bytes 524288 | tf_op jit(solution)/shard_map/all_to_all | solution.py:159
  22.9 0.3 shard_map.39
  23.1 0.0 copy-start.2
  23.2 33.5 %all_to_all.21.own = f32[8,256,256]{2,1,0:T(8,128)S(1)} all-to-all(f32[8,256,256]{2,1,0:T(8,128)S(1)} %shard_map.39), channel_id=1, replica_groups=mesh['planes'=8,'quads'=4,'cols'=8] {'cols'}, dimensions={0} | all-to-all | bytes 4194304 | tf_op jit(solution)/shard_map/all_to_all | solution.py:166
  56.7 0.0 copy-start.1
  56.7 0.0 collective-permute-start.5
  56.7 0.0 copy-done.2
  56.7 0.9 constant_dynamic-slice_fusion
  57.6 1.3 collective-permute-start.2
  58.9 0.9 collective-permute-start.1
  59.7 0.0 collective-permute-start
  59.8 0.1 pad_add_fusion.place
  59.8 6.1 %collective-permute-done.2.b3 = f32[2,128,256]{2,1,0:T(8,128)S(1)} collective-permute-done((f32[2,128,256]{2,1,0:T(8,128)}, f32[2,128,256]{2,1,0:T(8,128)S(1)}, u32[]{:S(2)}, u32[]{:S(2)}) %collective-permute-start.2) | collective-permute-done | bytes 262176 | tf_op jit(solution)/shard_map/ppermute | solution.py:164
  65.9 6.2 %collective-permute-done.1.b2 = f32[2,128,256]{2,1,0:T(8,128)S(1)} collective-permute-done((f32[2,128,256]{2,1,0:T(8,128)}, f32[2,128,256]{2,1,0:T(8,128)S(1)}, u32[]{:S(2)}, u32[]{:S(2)}) %collective-permute-start.1) | collective-permute-done | bytes 262176 | tf_op jit(solution)/shard_map/ppermute | solution.py:164
  72.1 0.0 collective-permute-done.b1
  72.1 0.6 shard_map.37
  72.7 1.2 collective-permute-start.3
  73.9 2.1 %collective-permute-start.4 = (f32[2,2,128,256]{3,2,1,0:T(8,128)S(1)}, f32[2,2,128,256]{3,2,1,0:T(8,128)S(1)}, u32[]{:S(2)}, u32[]{:S(2)}) collective-permute-start(f32[2,2,128,256]{3,2,1,0:T(8,128)S(1)} %get-tuple-element.8), channel_id=1, source_target_pairs={{0,224},{32,0},{64,32},{96,64},{128,96},{160,128},{192,160},{224,1... | collective-permute-start | bytes 1572872 | tf_op jit(solution)/shard_map/ppermute | solution.py:170
  76.0 10.8 %collective-permute-done.4.upper = f32[2,2,128,256]{3,2,1,0:T(8,128)S(1)} collective-permute-done((f32[2,2,128,256]{3,2,1,0:T(8,128)S(1)}, f32[2,2,128,256]{3,2,1,0:T(8,128)S(1)}, u32[]{:S(2)}, u32[]{:S(2)}) %collective-permute-start.4) | collective-permute-done | bytes 524320 | tf_op jit(solution)/shard_map/ppermute | solution.py:170
  86.9 11.6 %collective-permute-done.3.lower = f32[4,2,128,256]{3,2,1,0:T(8,128)S(1)} collective-permute-done((f32[4,2,128,256]{3,2,1,0:T(8,128)S(1)}, f32[4,2,128,256]{3,2,1,0:T(8,128)S(1)}, u32[]{:S(2)}, u32[]{:S(2)}) %collective-permute-start.3) | collective-permute-done | bytes 1048608 | tf_op jit(solution)/shard_map/ppermute | solution.py:169
  98.5 0.0 collective-permute-done.5.other
  98.5 0.0 copy-done.1
  98.5 4.2 %shard_map.40 = f32[4,2,128,256]{3,2,1,0:T(8,128)S(1)} custom-call(s32[4,4]{1,0:T(4,128)S(1)} %copy-done.1, s32[3]{0:T(128)S(1)} %pad_add_fusion.place, f32[4,2,128,256]{3,2,1,0:T(8,128)S(1)} %collective-permute-done.3.lower, f32[4,2,128,256]{3,2,1,0:T(8,128)S(1)} %get-tuple-element.7.middle, f32[2,2,128,256]{3,2,1,0:T(8,128)S(1)} %collective-permute-done.4.upper, ...), custom_call_target="tpu_custom_call" | custom-call | tf_op jit(solution)/shard_map/pallas_call | solution.py:173
  102.7 19.8 %all_to_all.22 = f32[32,32,256]{2,1,0:T(8,128)S(1)} all-to-all(f32[32,32,256]{2,1,0:T(8,128)S(1)} %bitcast.7), channel_id=1, replica_groups=mesh['planes'=8,'quads'=4,'cols'=8] {'quads','cols'}, dimensions={0} | all-to-all | bytes 2097152 | tf_op jit(solution)/shard_map/all_to_all | solution.py:177
  122.5 3.2 %shard_map.41 = f32[8,32,1024]{2,1,0:T(8,128)S(1)} custom-call(s32[4,4]{1,0:T(4,128)S(1)} %copy-done.1, s32[3]{0:T(128)S(1)} %pad_add_fusion.place, f32[4,8,32,256]{3,2,1,0:T(8,128)S(1)} %bitcast.8, f32[8,256,256]{2,1,0:T(8,128)S(1)} %all_to_all.21.own, f32[8,256,256]{2,1,0:T(8,128)} %collective-permute-done.5.other), custom_call_target="tpu_custom_call" | custom-call | tf_op jit(solution)/shard_map/pallas_call | solution.py:179
  125.7 21.1 %all_to_all.23 = f32[8,32,1024]{2,1,0:T(8,128)S(1)} all-to-all(f32[8,32,1024]{2,1,0:T(8,128)S(1)} %shard_map.41), channel_id=1, replica_groups=mesh['planes'=8,'quads'=4,'cols'=8] {'cols'}, dimensions={0} | all-to-all | bytes 2097152 | tf_op jit(solution)/shard_map/all_to_all | solution.py:182
  146.8 1.0 copy.5
Async XLA Ops:
  0.0 0.8 copy-start
  23.1 33.6 %copy-start.2 = (f32[256,1024]{1,0:T(8,128)S(1)}, f32[256,1024]{1,0:T(8,128)}, u32[]{:S(2)}) copy-start(f32[256,1024]{1,0:T(8,128)} %param.3) | copy-start | bytes 3145732
  56.7 41.8 %copy-start.1 = (s32[4,4]{1,0:T(4,128)S(1)}, s32[4,4]{1,0:T(4,128)}, u32[]{:S(2)}) copy-start(s32[4,4]{1,0:T(4,128)} %starts.3) | copy-start | bytes 196
  56.7 41.8 %collective-permute-start.5 = (f32[8,256,256]{2,1,0:T(8,128)S(1)}, f32[8,256,256]{2,1,0:T(8,128)}, u32[]{:S(2)}, u32[]{:S(2)}) collective-permute-start(f32[8,256,256]{2,1,0:T(8,128)S(1)} %all_to_all.21.own), channel_id=1, source_target_pairs={{0,8},{8,0},{16,24},{24,16},{1,9},{9,1},{17,25},{25,17},{2,10},{10... | collective-permute-start | bytes 6291464 | tf_op jit(solution)/shard_map/ppermute | solution.py:171
  57.6 8.3 %collective-permute-start.2 = (f32[2,128,256]{2,1,0:T(8,128)}, f32[2,128,256]{2,1,0:T(8,128)S(1)}, u32[]{:S(2)}, u32[]{:S(2)}) collective-permute-start(f32[2,128,256]{2,1,0:T(8,128)} %get-tuple-element.9), channel_id=1, source_target_pairs={{0,24},{8,16},{16,8},{24,0},{1,25},{9,17},{17,9},{25,1},{2,26},{10... | collective-permute-start | bytes 786440 | tf_op jit(solution)/shard_map/ppermute | solution.py:164
  58.9 13.2 %collective-permute-start.1 = (f32[2,128,256]{2,1,0:T(8,128)}, f32[2,128,256]{2,1,0:T(8,128)S(1)}, u32[]{:S(2)}, u32[]{:S(2)}) collective-permute-start(f32[2,128,256]{2,1,0:T(8,128)} %get-tuple-element.10), channel_id=1, source_target_pairs={{0,16},{8,24},{16,0},{24,8},{1,17},{9,25},{17,1},{25,9},{2,18},{10... | collective-permute-start | bytes 786440 | tf_op jit(solution)/shard_map/ppermute | solution.py:164
  59.7 12.3 %collective-permute-start = (f32[2,128,256]{2,1,0:T(8,128)}, f32[2,128,256]{2,1,0:T(8,128)S(1)}, u32[]{:S(2)}, u32[]{:S(2)}) collective-permute-start(f32[2,128,256]{2,1,0:T(8,128)} %get-tuple-element.11), channel_id=1, source_target_pairs={{0,8},{8,0},{16,24},{24,16},{1,9},{9,1},{17,25},{25,17},{2,10},{10... | collective-permute-start | bytes 786440 | tf_op jit(solution)/shard_map/ppermute | solution.py:164
  72.7 25.8 %collective-permute-start.3 = (f32[4,2,128,256]{3,2,1,0:T(8,128)S(1)}, f32[4,2,128,256]{3,2,1,0:T(8,128)S(1)}, u32[]{:S(2)}, u32[]{:S(2)}) collective-permute-start(f32[4,2,128,256]{3,2,1,0:T(8,128)S(1)} %get-tuple-element.7.middle), channel_id=1, source_target_pairs={{0,32},{32,64},{64,96},{96,128},{128,160},{160,192},{192,224},{224... | collective-permute-start | bytes 3145736 | tf_op jit(solution)/shard_map/ppermute | solution.py:169
  73.9 13.0 %collective-permute-start.4 = (f32[2,2,128,256]{3,2,1,0:T(8,128)S(1)}, f32[2,2,128,256]{3,2,1,0:T(8,128)S(1)}, u32[]{:S(2)}, u32[]{:S(2)}) collective-permute-start(f32[2,2,128,256]{3,2,1,0:T(8,128)S(1)} %get-tuple-element.8), channel_id=1, source_target_pairs={{0,224},{32,0},{64,32},{96,64},{128,96},{160,128},{192,160},{224,1... | collective-permute-start | bytes 1572872 | tf_op jit(solution)/shard_map/ppermute | solution.py:170
where the time goes:
time: 148 us
  blocking collectives  96.4 us (65%)
  waiting for transfers between devices  34.7 us (23%)
  Pallas kernels  8.37 us (6%)
  starting transfers between devices  5.44 us (4%)
  local copies, waits for them, and re-layouts  2.73 us (2%)
    all_to_all x1, blocking collectives, local(): own = lax.all_to_all(sent, 'cols', 0, 0, tiled=True)  33.5 us
    all_to_all x1, blocking collectives, local(): got = lax.all_to_all(sent, ('planes', 'quads'), 0, 0, tiled=True)  21.9 us
    all_to_all x1, blocking collectives, local(): home = lax.all_to_all(done, 'cols', 0, 0, tiled=True)  21.1 us
    all_to_all x1, blocking collectives, local(): came = lax.all_to_all(rows, ('quads', 'cols'), 0, 0, tiled=True)  19.8 us
    ppermute x3, waiting for transfers between devices, local(): lax.ppermute(quarters[m], 'quads', [(i, i ^ m) for i in range(QUADS)])  12.2 us
    ppermute x1, waiting for transfers between devices, local(): lax.ppermute(middle, 'planes', [(i, (i + 1) % PLANES) for i in range(PLAN...  11.6 us
    ppermute x1, waiting for transfers between devices, local(): lax.ppermute(low, 'planes', [(i, (i - 1) % PLANES) for i in range(PLANES)])  10.8 us
    pallas_call x1, Pallas kernels, local(): kernel(row_kernel, 2, 5, [panel], wide)  4.17 us
  transfers between devices with their start and end apart: 6, of which 4 were waited for; matrix products, arithmetic and copies ran while one was open for 1% of the time, Pallas kernels for 0%

commit v1 on v0

--- a/solution.py
+++ b/solution.py
@@ -108,12 +108,14 @@
 
     panel[1:5] = middle[...]
     row_pass(panel, plane, 0, 4, starts, core, own, other)
-    out[...] = panel[1:5]
+    for e in range(COLS):
+        at = e % 4 * EACH
+        out[e] = panel[1:5, e // 4, at : at + EACH, :]
 
 
 def col_kernel(starts, place, data, own, other, out):
     for q in range(QUADS):
-        out[:, :, q * WIDE : (q + 1) * WIDE] = data[q]
+        out[:, :, q * WIDE : (q + 1) * WIDE] = data[:, q]
 
     def spot(block):
         return lax.rem(block, COLS), pl.multiple_of(lax.div(block, COLS) * NB, NB)
@@ -170,12 +172,12 @@
     upper = lax.ppermute(low, "planes", [(i, (i - 1) % PLANES) for i in range(PLANES)])
     other = lax.ppermute(own, "quads", [(i, i ^ 1) for i in range(QUADS)])
     wide = [(QUADS + 2, 2, NB, WIDE), (QUADS + 1, 2, NB, WIDE)]
-    (rows,) = kernel(row_kernel, 2, 5, [panel], wide)(
+    (rows,) = kernel(row_kernel, 2, 5, [(COLS, QUADS, EACH, WIDE)], wide)(
         starts, place, lower, middle, upper, own, other
     )
     rows = rows.reshape(QUADS * COLS, EACH, WIDE)
-    came = lax.all_to_all(rows, ("quads", "cols"), 0, 0, tiled=True)
-    came = came.reshape(QUADS, COLS, EACH, WIDE)
+    came = lax.all_to_all(rows, ("cols", "quads"), 0, 0, tiled=True)
+    came = came.reshape(COLS, QUADS, EACH, WIDE)
     (done,) = kernel(col_kernel, 2, 3, [(COLS, EACH, QUADS * WIDE)])(
         starts, place, came, own, other
     )

time: 148 us -> 148 us (level)
  no operation moved by 1% of the time
where the time goes in v1:
time: 148 us; the launch traced here: 147 us
  blocking collectives  96.1 us (65%)
  waiting for transfers between devices  34.7 us (23%)
  Pallas kernels  8.37 us (6%)
  starting transfers between devices  5.44 us (4%)
  local copies, waits for them, and re-layouts  2.73 us (2%)
    all_to_all x1, blocking collectives, local(): own = lax.all_to_all(sent, 'cols', 0, 0, tiled=True)  33.5 us
    all_to_all x1, blocking collectives, local(): got = lax.all_to_all(sent, ('planes', 'quads'), 0, 0, tiled=True)  21.9 us
    all_to_all x1, blocking collectives, local(): home = lax.all_to_all(done, 'cols', 0, 0, tiled=True)  20.9 us
    all_to_all x1, blocking collectives, local(): came = lax.all_to_all(rows, ('cols', 'quads'), 0, 0, tiled=True)  19.7 us
    ppermute x3, waiting for transfers between devices, local(): lax.ppermute(quarters[m], 'quads', [(i, i ^ m) for i in range(QUADS)])  12.2 us
    ppermute x1, waiting for transfers between devices, local(): lax.ppermute(middle, 'planes', [(i, (i + 1) % PLANES) for i in range(PLAN...  11.6 us
    ppermute x1, waiting for transfers between devices, local(): lax.ppermute(low, 'planes', [(i, (i - 1) % PLANES) for i in range(PLANES)])  10.8 us
    pallas_call x1, Pallas kernels, local(): kernel(row_kernel, 2, 5, [(COLS, QUADS, EACH, WIDE)], wide)  4.17 us
  transfers between devices with their start and end apart: 6, of which 4 were waited for; matrix products, arithmetic and copies ran while one was open for 1% of the time, Pallas kernels for 0%

profile of v1, /device:TPU:8, one launch (start us, length us, event | category | flops | bytes accessed | tf_op | source)
XLA Modules:
  0.0 147.5 jit_solution(7257054845526097496)
XLA Ops:
  0.0 0.0 copy-start
  0.0 0.8 copy-done
  0.8 0.1 shard_map.38
  0.9 21.9 %all_to_all.20.pieces = f32[32,8,256]{2,1,0:T(8,128)S(1)} all-to-all(f32[32,8,256]{2,1,0:T(8,128)S(1)} %shard_map.38), channel_id=1, replica_groups=mesh['planes'=8,'quads'=4,'cols'=8] {'planes','quads'}, dimensions={0} | all-to-all | bytes 524288 | tf_op jit(solution)/shard_map/all_to_all | solution.py:161
  22.9 0.3 shard_map.39
  23.1 0.0 copy-start.2
  23.2 33.5 %all_to_all.21.own = f32[8,256,256]{2,1,0:T(8,128)S(1)} all-to-all(f32[8,256,256]{2,1,0:T(8,128)S(1)} %shard_map.39), channel_id=1, replica_groups=mesh['planes'=8,'quads'=4,'cols'=8] {'cols'}, dimensions={0} | all-to-all | bytes 4194304 | tf_op jit(solution)/shard_map/all_to_all | solution.py:168
  56.7 0.0 copy-start.1
  56.7 0.0 collective-permute-start.5
  56.7 0.0 copy-done.2
  56.7 0.9 constant_dynamic-slice_fusion
  57.6 1.3 collective-permute-start.2
  58.9 0.9 collective-permute-start.1
  59.7 0.0 collective-permute-start
  59.8 0.1 pad_add_fusion.place
  59.8 6.1 %collective-permute-done.2.b3 = f32[2,128,256]{2,1,0:T(8,128)S(1)} collective-permute-done((f32[2,128,256]{2,1,0:T(8,128)}, f32[2,128,256]{2,1,0:T(8,128)S(1)}, u32[]{:S(2)}, u32[]{:S(2)}) %collective-permute-start.2) | collective-permute-done | bytes 262176 | tf_op jit(solution)/shard_map/ppermute | solution.py:166
  65.9 6.2 %collective-permute-done.1.b2 = f32[2,128,256]{2,1,0:T(8,128)S(1)} collective-permute-done((f32[2,128,256]{2,1,0:T(8,128)}, f32[2,128,256]{2,1,0:T(8,128)S(1)}, u32[]{:S(2)}, u32[]{:S(2)}) %collective-permute-start.1) | collective-permute-done | bytes 262176 | tf_op jit(solution)/shard_map/ppermute | solution.py:166
  72.1 0.0 collective-permute-done.b1
  72.1 0.6 shard_map.37
  72.7 1.2 collective-permute-start.3
  73.9 2.1 %collective-permute-start.4 = (f32[2,2,128,256]{3,2,1,0:T(8,128)S(1)}, f32[2,2,128,256]{3,2,1,0:T(8,128)S(1)}, u32[]{:S(2)}, u32[]{:S(2)}) collective-permute-start(f32[2,2,128,256]{3,2,1,0:T(8,128)S(1)} %get-tuple-element.8), channel_id=1, source_target_pairs={{0,224},{32,0},{64,32},{96,64},{128,96},{160,128},{192,160},{224,1... | collective-permute-start | bytes 1572872 | tf_op jit(solution)/shard_map/ppermute | solution.py:172
  76.0 10.8 %collective-permute-done.4.upper = f32[2,2,128,256]{3,2,1,0:T(8,128)S(1)} collective-permute-done((f32[2,2,128,256]{3,2,1,0:T(8,128)S(1)}, f32[2,2,128,256]{3,2,1,0:T(8,128)S(1)}, u32[]{:S(2)}, u32[]{:S(2)}) %collective-permute-start.4) | collective-permute-done | bytes 524320 | tf_op jit(solution)/shard_map/ppermute | solution.py:172
  86.9 11.6 %collective-permute-done.3.lower = f32[4,2,128,256]{3,2,1,0:T(8,128)S(1)} collective-permute-done((f32[4,2,128,256]{3,2,1,0:T(8,128)S(1)}, f32[4,2,128,256]{3,2,1,0:T(8,128)S(1)}, u32[]{:S(2)}, u32[]{:S(2)}) %collective-permute-start.3) | collective-permute-done | bytes 1048608 | tf_op jit(solution)/shard_map/ppermute | solution.py:171
  98.5 0.0 collective-permute-done.5.other
  98.5 0.0 copy-done.1
  98.5 4.2 %shard_map.40 = f32[8,4,32,256]{3,2,1,0:T(8,128)S(1)} custom-call(s32[4,4]{1,0:T(4,128)S(1)} %copy-done.1, s32[3]{0:T(128)S(1)} %pad_add_fusion.place, f32[4,2,128,256]{3,2,1,0:T(8,128)S(1)} %collective-permute-done.3.lower, f32[4,2,128,256]{3,2,1,0:T(8,128)S(1)} %get-tuple-element.7.middle, f32[2,2,128,256]{3,2,1,0:T(8,128)S(1)} %collective-permute-done.4.upper, ...), custom_call_target="tpu_custom_call" | custom-call | tf_op jit(solution)/shard_map/pallas_call | solution.py:175
  102.7 19.7 %all_to_all.22 = f32[32,32,256]{2,1,0:T(8,128)S(1)} all-to-all(f32[32,32,256]{2,1,0:T(8,128)S(1)} %bitcast.7), channel_id=1, replica_groups=mesh['planes'=8,'quads'=4,'cols'=8] {'cols','quads'}, dimensions={0} | all-to-all | bytes 2097152 | tf_op jit(solution)/shard_map/all_to_all | solution.py:179
  122.4 3.2 %shard_map.41 = f32[8,32,1024]{2,1,0:T(8,128)S(1)} custom-call(s32[4,4]{1,0:T(4,128)S(1)} %copy-done.1, s32[3]{0:T(128)S(1)} %pad_add_fusion.place, f32[8,4,32,256]{3,2,1,0:T(8,128)S(1)} %bitcast.8, f32[8,256,256]{2,1,0:T(8,128)S(1)} %all_to_all.21.own, f32[8,256,256]{2,1,0:T(8,128)} %collective-permute-done.5.other), custom_call_target="tpu_custom_call" | custom-call | tf_op jit(solution)/shard_map/pallas_call | solution.py:181
  125.6 20.9 %all_to_all.23 = f32[8,32,1024]{2,1,0:T(8,128)S(1)} all-to-all(f32[8,32,1024]{2,1,0:T(8,128)S(1)} %shard_map.41), channel_id=1, replica_groups=mesh['planes'=8,'quads'=4,'cols'=8] {'cols'}, dimensions={0} | all-to-all | bytes 2097152 | tf_op jit(solution)/shard_map/all_to_all | solution.py:184
  146.5 1.0 copy.5
Async XLA Ops:
  0.0 0.8 copy-start
  23.1 33.6 %copy-start.2 = (f32[256,1024]{1,0:T(8,128)S(1)}, f32[256,1024]{1,0:T(8,128)}, u32[]{:S(2)}) copy-start(f32[256,1024]{1,0:T(8,128)} %param.3) | copy-start | bytes 3145732
  56.7 41.8 %copy-start.1 = (s32[4,4]{1,0:T(4,128)S(1)}, s32[4,4]{1,0:T(4,128)}, u32[]{:S(2)}) copy-start(s32[4,4]{1,0:T(4,128)} %starts.3) | copy-start | bytes 196
  56.7 41.8 %collective-permute-start.5 = (f32[8,256,256]{2,1,0:T(8,128)S(1)}, f32[8,256,256]{2,1,0:T(8,128)}, u32[]{:S(2)}, u32[]{:S(2)}) collective-permute-start(f32[8,256,256]{2,1,0:T(8,128)S(1)} %all_to_all.21.own), channel_id=1, source_target_pairs={{0,8},{8,0},{16,24},{24,16},{1,9},{9,1},{17,25},{25,17},{2,10},{10... | collective-permute-start | bytes 6291464 | tf_op jit(solution)/shard_map/ppermute | solution.py:173
  57.6 8.3 %collective-permute-start.2 = (f32[2,128,256]{2,1,0:T(8,128)}, f32[2,128,256]{2,1,0:T(8,128)S(1)}, u32[]{:S(2)}, u32[]{:S(2)}) collective-permute-start(f32[2,128,256]{2,1,0:T(8,128)} %get-tuple-element.9), channel_id=1, source_target_pairs={{0,24},{8,16},{16,8},{24,0},{1,25},{9,17},{17,9},{25,1},{2,26},{10... | collective-permute-start | bytes 786440 | tf_op jit(solution)/shard_map/ppermute | solution.py:166
  58.9 13.2 %collective-permute-start.1 = (f32[2,128,256]{2,1,0:T(8,128)}, f32[2,128,256]{2,1,0:T(8,128)S(1)}, u32[]{:S(2)}, u32[]{:S(2)}) collective-permute-start(f32[2,128,256]{2,1,0:T(8,128)} %get-tuple-element.10), channel_id=1, source_target_pairs={{0,16},{8,24},{16,0},{24,8},{1,17},{9,25},{17,1},{25,9},{2,18},{10... | collective-permute-start | bytes 786440 | tf_op jit(solution)/shard_map/ppermute | solution.py:166
  59.7 12.3 %collective-permute-start = (f32[2,128,256]{2,1,0:T(8,128)}, f32[2,128,256]{2,1,0:T(8,128)S(1)}, u32[]{:S(2)}, u32[]{:S(2)}) collective-permute-start(f32[2,128,256]{2,1,0:T(8,128)} %get-tuple-element.11), channel_id=1, source_target_pairs={{0,8},{8,0},{16,24},{24,16},{1,9},{9,1},{17,25},{25,17},{2,10},{10... | collective-permute-start | bytes 786440 | tf_op jit(solution)/shard_map/ppermute | solution.py:166
  72.7 25.8 %collective-permute-start.3 = (f32[4,2,128,256]{3,2,1,0:T(8,128)S(1)}, f32[4,2,128,256]{3,2,1,0:T(8,128)S(1)}, u32[]{:S(2)}, u32[]{:S(2)}) collective-permute-start(f32[4,2,128,256]{3,2,1,0:T(8,128)S(1)} %get-tuple-element.7.middle), channel_id=1, source_target_pairs={{0,32},{32,64},{64,96},{96,128},{128,160},{160,192},{192,224},{224... | collective-permute-start | bytes 3145736 | tf_op jit(solution)/shard_map/ppermute | solution.py:171
  73.9 13.0 %collective-permute-start.4 = (f32[2,2,128,256]{3,2,1,0:T(8,128)S(1)}, f32[2,2,128,256]{3,2,1,0:T(8,128)S(1)}, u32[]{:S(2)}, u32[]{:S(2)}) collective-permute-start(f32[2,2,128,256]{3,2,1,0:T(8,128)S(1)} %get-tuple-element.8), channel_id=1, source_target_pairs={{0,224},{32,0},{64,32},{96,64},{128,96},{160,128},{192,160},{224,1... | collective-permute-start | bytes 1572872 | tf_op jit(solution)/shard_map/ppermute | solution.py:172
